TPU v7x, 32 devices: a whole 2x2x4 slice. The times are simulated.
32 devices in a mesh: lib: 2 (over y), row: 4 (over z), col: 4 (over x, core).
Axes of the slice: x: 2, y: 2, z: 4, core: 2. Of those that a mesh axis runs over, the one named last changes fastest.
Arguments:
- abundance: float32 [1024, 128, 1024], P('lib', 'row', 'col'), may hold values from 0 to 1
- duals: float32 [2, 1024, 128, 1024], P(None, 'lib', 'row', 'col'), may hold values from -1 to 1
- reflectance: bfloat16 [224, 128, 1024], P(None, 'row', 'col'), may hold values from -6 to 6
- library: bfloat16 [224, 1024], P(None, 'lib'), may hold values from -0.375 to 0.375
Outputs:
- abund_next: float32 [1024, 128, 1024], P('lib', 'row', 'col')
- duals_next: float32 [2, 1024, 128, 1024], P(None, 'lib', 'row', 'col')
All inputs are finite; a program needn't handle non-finite values.
Results may differ from a plain program's by a relative error of at most 0.0018.
Values may be sent and summed in bfloat16 or wider, within the bound.
A program may use at most 384 MiB of HBM per device.

v0:
```python
import jax
import jax.numpy as jnp
from jax import lax
from jax.sharding import PartitionSpec as P

PASSES = 3


def for_sending(array):
    return jax.tree.map(lambda a: a.astype(jnp.bfloat16) if a.dtype == jnp.float32 else a, array)


def shifted(array, axis, by):
    length = lax.axis_size(axis)
    pairs = [(i, i + by) for i in range(length) if 0 <= i + by < length]
    return lax.ppermute(array, axis, pairs)


def on_device(abundance, duals, reflectance, library):
    maps, height, width = abundance.shape
    bands = library.shape[0]
    pixels = height * width
    total_rows = height * lax.axis_size("row")
    total_cols = width * lax.axis_size("col")
    row_place = lax.axis_index("row") * height + lax.broadcasted_iota(jnp.int32, (height, width), 0)
    col_place = lax.axis_index("col") * width + lax.broadcasted_iota(jnp.int32, (height, width), 1)
    keep_rows = (row_place < total_rows - 1).astype(jnp.float32)
    keep_cols = (col_place < total_cols - 1).astype(jnp.float32)
    dual = jnp.stack([duals[0] * keep_rows, duals[1] * keep_cols])
    compact = abundance.astype(jnp.bfloat16).reshape(maps, pixels)
    observed = reflectance.reshape(bands, pixels).astype(jnp.float32)
    partial_value = jnp.dot(library, compact, preferred_element_type=jnp.float32)
    resid = lax.psum(partial_value, "lib") - observed
    descent = jnp.einsum(
        "bm,bp->mp", library, resid.astype(jnp.bfloat16), preferred_element_type=jnp.float32
    )
    start = abundance - 0.1 * descent.reshape(maps, height, width)

    def inner_field(current):
        above = shifted(for_sending(current[0][:, height - 1 :, :]), "row", 1)
        left = shifted(current[1][:, :, width - 1 :], "col", 1)
        first_prev = jnp.concatenate([above, current[0][:, : height - 1, :]], axis=1)
        second_prev = jnp.concatenate([left, current[1][:, :, : width - 1]], axis=2)
        return start - 0.25 * (current[0] - first_prev + (current[1] - second_prev))

    for step in range(PASSES):
        field = inner_field(dual)
        below = shifted(for_sending(field[:, :1, :]), "row", -1)
        beside = shifted(field[:, :, :1], "col", -1)
        down = (jnp.concatenate([field[:, 1:, :], below], axis=1) - field) * keep_rows
        right = (jnp.concatenate([field[:, :, 1:], beside], axis=2) - field) * keep_cols
        dual = jnp.clip(dual + 0.5 * jnp.stack([down, right]), -1.0, 1.0)
    final = inner_field(dual)
    abund_next = jnp.maximum(final - 0.02, 0.0)
    return (abund_next, dual)


def solution(mesh):
    placed = (
        P("lib", "row", "col"),
        P(None, "lib", "row", "col"),
        P(None, "row", "col"),
        P(None, "lib"),
    )
    return jax.shard_map(
        on_device,
        mesh=mesh,
        in_specs=placed,
        out_specs=(P("lib", "row", "col"), P(None, "lib", "row", "col")),
        check_vma=False,
    )
```

profile of v0, /device:TPU:1, one launch (start us, length us, event | category | flops | bytes accessed | tf_op | source)
XLA Modules:
  0.0 879.3 jit_solution(16934538867527394651)
XLA Ops:
  7.2 9.1 %convert_element_type.50 = bf16[512,32,256]{2,1,0:T(8,128)(2,1)} convert(f32[512,32,256]{2,1,0:T(8,128)} %param.4) | non-fusion elementwise | flops 4194304 | bytes 25165824 | tf_op jit(solution)/shard_map/convert_element_type | solution.py:30
  16.3 16.6 %copy.15 = bf16[64,8,32,256]{3,1,2,0:T(8,128)(2,1)} copy(bf16[64,8,32,256]{3,2,1,0:T(8,128)(2,1)} %bitcast.71) | data formatting | bytes 16777216
  33.0 8.7 fusion.32
  41.7 22.1 %fusion.31 = (f32[1,512,32,256]{3,2,1,0:T(8,128)}, f32[1,512,32,256]{3,2,1,0:T(8,128)}) fusion(f32[2,512,32,256]{3,2,1,0:T(8,128)} %param.5), kind=kLoop, calls=%fused_computation.71 | loop fusion | bytes 67108864 | tf_op jit(solution)/shard_map/slice | solution.py:29
  63.8 20.3 %copy.13 = f32[1,512,32,256]{1,2,3,0:T(8,128)} copy(f32[1,512,32,256]{3,2,1,0:T(8,128)} %get-tuple-element.13) | data formatting | bytes 33554432
  102.6 20.2 %copy.14 = f32[1,512,32,256]{1,2,3,0:T(8,128)} copy(f32[1,512,32,256]{3,2,1,0:T(8,128)} %get-tuple-element.12) | data formatting | bytes 33554432
  130.9 8.3 copy-done.7
  149.5 20.5 %copy.7 = f32[512,32,256]{0,1,2:T(8,128)} copy(f32[512,32,256]{2,1,0:T(8,128)} %param.4) | data formatting | bytes 33554432 | tf_op args[0]
  170.0 12.5 %slice.166 = f32[512,32,255]{0,1,2:T(8,128)} slice(f32[512,32,256]{0,1,2:T(8,128)} %copy-done.7), slice={[0:512], [0:32], [0:255]} | slice | bytes 33423360 | tf_op jit(solution)/shard_map/slice | solution.py:43
  189.3 30.4 %all-reduce.2.cloned.1.call-done = f32[224,8192]{1,0:T(8,128)} async-done(((f32[224,8192]{1,0:T(8,128)}), f32[224,8192]{1,0:T(8,128)}) %all-reduce.2.cloned.1.call-update) | async-done | bytes 7340048 | tf_op jit(solution)/shard_map/psum | solution.py:33
  219.7 13.8 %convolution_multiply_fusion = f32[8192,512]{1,0:T(8,128)} fusion(bf16[224,512]{1,0:T(8,128)(2,1)S(1)} %copy-done, f32[224,8192]{1,0:T(8,128)} %all-reduce.2.cloned.1.call-done, f32[224,8192]{1,0:T(8,128)} %bitcast.70), kind=kOutput, calls=%fused_computation.58 | convolution fusion | flops 1886912512 | bytes 31686656 | tf_op jit(solution)/shard_map/bm,bp->mp/dot_general | solution.py:34
  233.5 47.7 %fusion.7 = (f32[512,32,256]{0,1,2:T(8,128)}, f32[512,32,256]{0,1,2:T(8,128)}) fusion(f32[512,31,256]{0,1,2:T(8,128)} %bitcast.66, f32[512,1,256]{0,1,2:T(1,128)S(1)} %convert_element_type.56, f32[512,32,255]{0,1,2:T(8,128)} %slice.166, f32[512,32,1]{0,1,2:T(8,128)S(1)} %collective-permute-done.1, f32[512,32,256]{0,1,2:T(8,128)} %copy.7, ...), kind=kLoop, calls=%fused_computation.18 | loop fusion | flops 41943040 | bytes 134218880 | tf_op jit(solution)/shard_map/sub | solution.py:44
  289.5 12.0 %broadcast_multiply_fusion.1 = f32[1,512,32,256]{1,2,3,0:T(8,128)} fusion(f32[1,512,32,256]{1,2,3,0:T(8,128)} %copy.13, f32[32]{0:T(128)S(1)} %compare_convert_fusion.1), kind=kLoop, calls=%fused_computation.60 | loop fusion | flops 4194304 | bytes 33554560 | tf_op jit(solution)/shard_map/mul | solution.py:29
  316.6 27.8 %fusion.9 = (f32[1,512,32,256]{1,2,3,0:T(8,128)}, f32[1,512,32,256]{1,2,3,0:T(8,128)}) fusion(f32[512,32,256]{0,1,2:T(8,128)} %get-tuple-element.4, f32[512,1,256]{0,1,2:T(1,128)S(1)} %convert_element_type.57, f32[512,31,256]{0,1,2:T(8,128)} %slice.167, f32[32]{0:T(128)S(1)} %compare_convert_fusion.1, f32[256]{0:T(256)S(1)} %compare_convert_fusion, ...), kind=kLoop, calls=%fused_computation.22 | loop fusion | flops 25165824 | bytes 83887232 | tf_op jit(solution)/shard_map/stack | solution.py:52
  344.3 33.4 %fusion = f32[2,512,32,256]{1,2,3,0:T(8,128)} fusion(f32[1,512,32,256]{1,2,3,0:T(8,128)} %broadcast_multiply_fusion, f32[1,512,32,256]{1,2,3,0:T(8,128)} %broadcast_multiply_fusion.1, f32[1,512,32,256]{1,2,3,0:T(8,128)} %get-tuple-element.19, f32[1,512,32,256]{1,2,3,0:T(8,128)} %get-tuple-element.18), kind=kLoop, calls=%fused_computation.1 | loop fusion | flops 41943040 | bytes 100663296 | tf_op jit(solution)/shard_map/jit(clip)/min | solution.py:52
  377.8 17.2 %slice_bitcast_fusion.4 = (f32[512,32,256]{0,1,2:T(8,128)}, f32[512,32,256]{0,1,2:T(8,128)S(1)}) fusion(f32[2,512,32,256]{1,2,3,0:T(8,128)} %fusion), kind=kLoop, calls=%fused_computation.13 | loop fusion | bytes 67108864 | tf_op jit(solution)/shard_map/squeeze | solution.py:44
  404.2 11.7 %slice.176 = f32[512,32,255]{0,1,2:T(8,128)} slice(f32[512,32,256]{0,1,2:T(8,128)} %get-tuple-element.10), slice={[0:512], [0:32], [0:255]} | slice | bytes 33423360 | tf_op jit(solution)/shard_map/slice | solution.py:43
  416.5 34.5 %fusion.14 = f32[512,32,256]{0,1,2:T(8,128)} fusion(f32[512,32,256]{0,1,2:T(8,128)} %get-tuple-element.5, f32[512,31,256]{0,1,2:T(8,128)} %bitcast.68, f32[512,1,256]{0,1,2:T(1,128)S(1)} %convert_element_type.58, f32[512,32,255]{0,1,2:T(8,128)} %slice.176, f32[512,32,1]{0,1,2:T(8,128)S(1)} %collective-permute-done.5, f32[2,512,32,256]{1,2,3,0:T(8,128)} %fusion), kind=kLoop, calls=%fused_computation.29 | loop fusion | flops 29360128 | bytes 100663296 | tf_op jit(solution)/shard_map/sub | solution.py:44
  458.4 12.7 %slice.179 = f32[512,32,255]{0,1,2:T(8,128)} slice(f32[512,32,256]{0,1,2:T(8,128)} %fusion.14), slice={[0:512], [0:32], [1:256]} | slice | bytes 33423360 | tf_op jit(solution)/shard_map/slice | solution.py:51
  479.1 27.7 %fusion.16 = (f32[1,512,32,256]{1,2,3,0:T(8,128)}, f32[1,512,32,256]{1,2,3,0:T(8,128)}) fusion(f32[512,32,256]{0,1,2:T(8,128)} %fusion.14, f32[512,1,256]{0,1,2:T(1,128)S(1)} %convert_element_type.59, f32[512,31,256]{0,1,2:T(8,128)} %slice.177, f32[32]{0:T(128)S(1)} %compare_convert_fusion.1, f32[256]{0:T(256)S(1)} %compare_convert_fusion, ...), kind=kLoop, calls=%fused_computation.33 | loop fusion | flops 25165824 | bytes 83887232 | tf_op jit(solution)/shard_map/stack | solution.py:52
  506.7 43.8 %fusion.2 = f32[2,512,32,256]{1,2,3,0:T(8,128)} fusion(f32[1,512,32,256]{1,2,3,0:T(8,128)} %get-tuple-element.17, f32[1,512,32,256]{1,2,3,0:T(8,128)} %get-tuple-element.16, f32[1,512,32,256]{1,2,3,0:T(8,128)} %get-tuple-element.19, f32[1,512,32,256]{1,2,3,0:T(8,128)} %get-tuple-element.18, f32[1,512,32,256]{1,2,3,0:T(8,128)} %broadcast_multiply_fusion, ...), kind=kLoop, calls=%fused_computation.5 | loop fusion | flops 75497472 | bytes 134217728 | tf_op jit(solution)/shard_map/jit(clip)/min | solution.py:52
  550.6 17.2 %slice_bitcast_fusion.2 = (f32[512,32,256]{0,1,2:T(8,128)}, f32[512,32,256]{0,1,2:T(8,128)S(1)}) fusion(f32[2,512,32,256]{1,2,3,0:T(8,128)} %fusion.2), kind=kLoop, calls=%fused_computation.11 | loop fusion | bytes 67108864 | tf_op jit(solution)/shard_map/squeeze | solution.py:44
  576.4 11.7 %slice.186 = f32[512,32,255]{0,1,2:T(8,128)} slice(f32[512,32,256]{0,1,2:T(8,128)} %get-tuple-element.8), slice={[0:512], [0:32], [0:255]} | slice | bytes 33423360 | tf_op jit(solution)/shard_map/slice | solution.py:43
  588.6 34.4 %fusion.21 = f32[512,32,256]{0,1,2:T(8,128)} fusion(f32[512,32,256]{0,1,2:T(8,128)} %get-tuple-element.5, f32[512,31,256]{0,1,2:T(8,128)} %bitcast.69, f32[512,1,256]{0,1,2:T(1,128)S(1)} %convert_element_type.60, f32[512,32,255]{0,1,2:T(8,128)} %slice.186, f32[512,32,1]{0,1,2:T(8,128)S(1)} %collective-permute-done.9, f32[2,512,32,256]{1,2,3,0:T(8,128)} %fusion.2), kind=kLoop, calls=%fused_computation.40 | loop fusion | flops 29360128 | bytes 100663296 | tf_op jit(solution)/shard_map/sub | solution.py:44
  630.5 12.8 %slice.189 = f32[512,32,255]{0,1,2:T(8,128)} slice(f32[512,32,256]{0,1,2:T(8,128)} %fusion.21), slice={[0:512], [0:32], [1:256]} | slice | bytes 33423360 | tf_op jit(solution)/shard_map/slice | solution.py:51
  651.2 27.6 %fusion.23 = (f32[1,512,32,256]{1,2,3,0:T(8,128)}, f32[1,512,32,256]{1,2,3,0:T(8,128)}) fusion(f32[512,32,256]{0,1,2:T(8,128)} %fusion.21, f32[512,1,256]{0,1,2:T(1,128)S(1)} %convert_element_type.61, f32[512,31,256]{0,1,2:T(8,128)} %slice.187, f32[32]{0:T(128)S(1)} %compare_convert_fusion.1, f32[256]{0:T(256)S(1)} %compare_convert_fusion, ...), kind=kLoop, calls=%fused_computation.44 | loop fusion | flops 25165824 | bytes 83887232 | tf_op jit(solution)/shard_map/stack | solution.py:52
  678.9 54.6 %fusion.4 = f32[2,512,32,256]{1,2,3,0:T(8,128)} fusion(f32[1,512,32,256]{1,2,3,0:T(8,128)} %get-tuple-element.15, f32[1,512,32,256]{1,2,3,0:T(8,128)} %get-tuple-element.14, f32[1,512,32,256]{1,2,3,0:T(8,128)} %get-tuple-element.17, f32[1,512,32,256]{1,2,3,0:T(8,128)} %get-tuple-element.16, f32[1,512,32,256]{1,2,3,0:T(8,128)} %get-tuple-element.19, ...), kind=kLoop, calls=%fused_computation.8 | loop fusion | flops 109051904 | bytes 167772160 | tf_op jit(solution)/shard_map/jit(clip)/min | solution.py:52
  733.5 17.3 %slice_bitcast_fusion = (f32[512,32,256]{0,1,2:T(8,128)}, f32[512,32,256]{0,1,2:T(8,128)S(1)}) fusion(f32[2,512,32,256]{1,2,3,0:T(8,128)} %fusion.4), kind=kLoop, calls=%fused_computation.9 | loop fusion | bytes 67108864 | tf_op jit(solution)/shard_map/squeeze | solution.py:44
  765.1 40.0 %copy.12 = f32[2,512,32,256]{3,2,1,0:T(8,128)} copy(f32[2,512,32,256]{1,2,3,0:T(8,128)} %fusion.4) | data formatting | bytes 67108864
  805.0 11.7 %slice.196 = f32[512,32,255]{0,1,2:T(8,128)} slice(f32[512,32,256]{0,1,2:T(8,128)} %get-tuple-element.6), slice={[0:512], [0:32], [0:255]} | slice | bytes 33423360 | tf_op jit(solution)/shard_map/slice | solution.py:43
  817.3 34.5 %fusion.30 = f32[512,32,256]{0,1,2:T(8,128)} fusion(f32[512,32,256]{0,1,2:T(8,128)} %get-tuple-element.5, f32[512,31,256]{0,1,2:T(8,128)} %bitcast.67, f32[512,1,256]{0,1,2:T(1,128)S(1)} %convert_element_type.62, f32[512,32,255]{0,1,2:T(8,128)} %slice.196, f32[512,32,1]{0,1,2:T(8,128)S(1)} %collective-permute-done.13, f32[2,512,32,256]{1,2,3,0:T(8,128)} %fusion.4), kind=kLoop, calls=%fused_computation.53 | loop fusion | flops 37748736 | bytes 100663296 | tf_op jit(solution)/shard_map/max | solution.py:54
  851.8 20.2 %copy.11 = f32[512,32,256]{2,1,0:T(8,128)} copy(f32[512,32,256]{0,1,2:T(8,128)} %fusion.30) | data formatting | bytes 33554432
  (105 shorter events, 131.2 us)
Async XLA Ops:
  7.2 25.8 %copy-start = (bf16[224,512]{1,0:T(8,128)(2,1)S(1)}, bf16[224,512]{1,0:T(8,128)(2,1)}, u32[]{:S(2)}) copy-start(bf16[224,512]{1,0:T(8,128)(2,1)} %param.7) | copy-start | bytes 688132
  7.2 212.5 %all-reduce.2.cloned.1.call-start = ((), (), s32[]{:S(2)}) async-start(), calls=%async_computation | async-start | bytes 14680064 | tf_op jit(solution)/shard_map/psum | solution.py:33
  98.4 90.4 %collective-permute-start = (bf16[512,1,256]{0,1,2:T(2,128)(2,1)S(1)}, bf16[512,1,256]{0,1,2:T(2,128)(2,1)S(1)}, u32[]{:S(2)}, u32[]{:S(2)}) collective-permute-start(bf16[512,1,256]{0,1,2:T(2,128)(2,1)S(1)} %slice.228), channel_id=1, source_target_pairs={{0,4},{4,8},{8,12},{1,5},{5,9},{9,13},{2,6},{6,10},{10,14},{3,7},{... | collective-permute-start | bytes 786440 | tf_op jit(solution)/shard_map/ppermute | solution.py:16
  122.9 20.3 %copy-start.2 = (f32[1,512,32,256]{1,2,3,0:T(8,128)S(1)}, f32[1,512,32,256]{1,2,3,0:T(8,128)}, u32[]{:S(2)}) copy-start(f32[1,512,32,256]{1,2,3,0:T(8,128)} %copy.14) | copy-start | bytes 50331652
  139.1 94.4 %collective-permute-start.1 = (f32[512,32,1]{0,1,2:T(8,128)S(1)}, f32[512,32,1]{0,1,2:T(8,128)S(1)}, u32[]{:S(2)}, u32[]{:S(2)}) collective-permute-start(f32[512,32,1]{0,1,2:T(8,128)S(1)} %slice.165), channel_id=1, source_target_pairs={{0,1},{1,2},{2,3},{4,5},{5,6},{6,7},{8,9},{9,10},{10,11},{12,13},{... | collective-permute-start | bytes 196616 | tf_op jit(solution)/shard_map/ppermute | solution.py:16
  282.1 19.5 %slice-start = ((s8[16777216]{0:T(1024)(128)(4,1)}), s8[4194304]{0:T(1024)(128)(4,1)S(1)}, s32[]{:S(2)}) async-start(s8[16777216]{0:T(1024)(128)(4,1)} %bitcast.59), calls=%async_computation.1 | async-start | bytes 8388608
  284.9 16.7 %slice-start.1 = ((s8[16777216]{0:T(1024)(128)(4,1)}), s8[4194304]{0:T(1024)(128)(4,1)S(1)}, s32[]{:S(2)}) async-start(s8[16777216]{0:T(1024)(128)(4,1)} %bitcast.59), calls=%async_computation.2 | async-start | bytes 8388608
  284.9 16.7 %slice-start.2 = ((s8[16777216]{0:T(1024)(128)(4,1)}), s8[4194304]{0:T(1024)(128)(4,1)S(1)}, s32[]{:S(2)}) async-start(s8[16777216]{0:T(1024)(128)(4,1)} %bitcast.59), calls=%async_computation.3 | async-start | bytes 8388608
  284.9 16.6 %slice-start.3 = ((s8[16777216]{0:T(1024)(128)(4,1)}), s8[4194304]{0:T(1024)(128)(4,1)S(1)}, s32[]{:S(2)}) async-start(s8[16777216]{0:T(1024)(128)(4,1)} %bitcast.59), calls=%async_computation.4 | async-start | bytes 8388608
  285.0 31.6 %collective-permute-start.3 = (f32[512,32,1]{0,1,2:T(8,128)S(1)}, f32[512,32,1]{0,1,2:T(8,128)S(1)}, u32[]{:S(2)}, u32[]{:S(2)}) collective-permute-start(f32[512,32,1]{0,1,2:T(8,128)S(1)} %slice.170), channel_id=1, source_target_pairs={{1,0},{2,1},{3,2},{5,4},{6,5},{7,6},{9,8},{10,9},{11,10},{13,12},{... | collective-permute-start | bytes 196616 | tf_op jit(solution)/shard_map/ppermute | solution.py:16
  288.1 27.9 %collective-permute-start.2 = (bf16[512,1,256]{0,1,2:T(2,128)(2,1)S(1)}, bf16[512,1,256]{0,1,2:T(2,128)(2,1)S(1)}, u32[]{:S(2)}, u32[]{:S(2)}) collective-permute-start(bf16[512,1,256]{0,1,2:T(2,128)(2,1)S(1)} %slice.227), channel_id=1, source_target_pairs={{4,0},{8,4},{12,8},{5,1},{9,5},{13,9},{6,2},{10,6},{14,10},{7,3},{... | collective-permute-start | bytes 786440 | tf_op jit(solution)/shard_map/ppermute | solution.py:16
  395.0 20.9 %copy-start.5 = (f32[512,32,256]{0,1,2:T(8,128)}, f32[512,32,256]{0,1,2:T(8,128)S(1)}, u32[]{:S(2)}) copy-start(f32[512,32,256]{0,1,2:T(8,128)S(1)} %get-tuple-element.11) | copy-start | bytes 50331652
  395.6 20.3 %collective-permute-start.4 = (bf16[512,1,256]{0,1,2:T(2,128)(2,1)S(1)}, bf16[512,1,256]{0,1,2:T(2,128)(2,1)S(1)}, u32[]{:S(2)}, u32[]{:S(2)}) collective-permute-start(bf16[512,1,256]{0,1,2:T(2,128)(2,1)S(1)} %slice.226), channel_id=1, source_target_pairs={{0,4},{4,8},{8,12},{1,5},{5,9},{9,13},{2,6},{6,10},{10,14},{3,7},{... | collective-permute-start | bytes 786440 | tf_op jit(solution)/shard_map/ppermute | solution.py:16
  400.5 15.9 %collective-permute-start.5 = (f32[512,32,1]{0,1,2:T(8,128)S(1)}, f32[512,32,1]{0,1,2:T(8,128)S(1)}, u32[]{:S(2)}, u32[]{:S(2)}) collective-permute-start(f32[512,32,1]{0,1,2:T(8,128)S(1)} %slice.175), channel_id=1, source_target_pairs={{0,1},{1,2},{2,3},{4,5},{5,6},{6,7},{8,9},{9,10},{10,11},{12,13},{... | collective-permute-start | bytes 196616 | tf_op jit(solution)/shard_map/ppermute | solution.py:16
  453.6 17.5 %slice-start.8 = ((s8[16777216]{0:T(1024)(128)(4,1)}), s8[4194304]{0:T(1024)(128)(4,1)S(1)}, s32[]{:S(2)}) async-start(s8[16777216]{0:T(1024)(128)(4,1)} %bitcast.63), calls=%async_computation.9 | async-start | bytes 8388608
  453.6 24.9 %collective-permute-start.6 = (bf16[512,1,256]{0,1,2:T(2,128)(2,1)S(1)}, bf16[512,1,256]{0,1,2:T(2,128)(2,1)S(1)}, u32[]{:S(2)}, u32[]{:S(2)}) collective-permute-start(bf16[512,1,256]{0,1,2:T(2,128)(2,1)S(1)} %slice.225), channel_id=1, source_target_pairs={{4,0},{8,4},{12,8},{5,1},{9,5},{13,9},{6,2},{10,6},{14,10},{7,3},{... | collective-permute-start | bytes 786440 | tf_op jit(solution)/shard_map/ppermute | solution.py:16
  456.0 15.1 %slice-start.9 = ((s8[16777216]{0:T(1024)(128)(4,1)}), s8[4194304]{0:T(1024)(128)(4,1)S(1)}, s32[]{:S(2)}) async-start(s8[16777216]{0:T(1024)(128)(4,1)} %bitcast.63), calls=%async_computation.10 | async-start | bytes 8388608
  456.1 15.1 %slice-start.10 = ((s8[16777216]{0:T(1024)(128)(4,1)}), s8[4194304]{0:T(1024)(128)(4,1)S(1)}, s32[]{:S(2)}) async-start(s8[16777216]{0:T(1024)(128)(4,1)} %bitcast.63), calls=%async_computation.11 | async-start | bytes 8388608
  456.1 15.1 %slice-start.11 = ((s8[16777216]{0:T(1024)(128)(4,1)}), s8[4194304]{0:T(1024)(128)(4,1)S(1)}, s32[]{:S(2)}) async-start(s8[16777216]{0:T(1024)(128)(4,1)} %bitcast.63), calls=%async_computation.12 | async-start | bytes 8388608
  456.1 23.0 %collective-permute-start.7 = (f32[512,32,1]{0,1,2:T(8,128)S(1)}, f32[512,32,1]{0,1,2:T(8,128)S(1)}, u32[]{:S(2)}, u32[]{:S(2)}) collective-permute-start(f32[512,32,1]{0,1,2:T(8,128)S(1)} %slice.180), channel_id=1, source_target_pairs={{1,0},{2,1},{3,2},{5,4},{6,5},{7,6},{9,8},{10,9},{11,10},{13,12},{... | collective-permute-start | bytes 196616 | tf_op jit(solution)/shard_map/ppermute | solution.py:16
  567.8 20.3 %copy-start.6 = (f32[512,32,256]{0,1,2:T(8,128)}, f32[512,32,256]{0,1,2:T(8,128)S(1)}, u32[]{:S(2)}) copy-start(f32[512,32,256]{0,1,2:T(8,128)S(1)} %get-tuple-element.9) | copy-start | bytes 50331652
  568.4 19.7 %collective-permute-start.8 = (bf16[512,1,256]{0,1,2:T(2,128)(2,1)S(1)}, bf16[512,1,256]{0,1,2:T(2,128)(2,1)S(1)}, u32[]{:S(2)}, u32[]{:S(2)}) collective-permute-start(bf16[512,1,256]{0,1,2:T(2,128)(2,1)S(1)} %slice.224), channel_id=1, source_target_pairs={{0,4},{4,8},{8,12},{1,5},{5,9},{9,13},{2,6},{6,10},{10,14},{3,7},{... | collective-permute-start | bytes 786440 | tf_op jit(solution)/shard_map/ppermute | solution.py:16
  573.3 15.3 %collective-permute-start.9 = (f32[512,32,1]{0,1,2:T(8,128)S(1)}, f32[512,32,1]{0,1,2:T(8,128)S(1)}, u32[]{:S(2)}, u32[]{:S(2)}) collective-permute-start(f32[512,32,1]{0,1,2:T(8,128)S(1)} %slice.185), channel_id=1, source_target_pairs={{0,1},{1,2},{2,3},{4,5},{5,6},{6,7},{8,9},{9,10},{10,11},{12,13},{... | collective-permute-start | bytes 196616 | tf_op jit(solution)/shard_map/ppermute | solution.py:16
  625.8 17.5 %slice-start.4 = ((s8[16777216]{0:T(1024)(128)(4,1)}), s8[4194304]{0:T(1024)(128)(4,1)S(1)}, s32[]{:S(2)}) async-start(s8[16777216]{0:T(1024)(128)(4,1)} %bitcast.61), calls=%async_computation.5 | async-start | bytes 8388608
  625.8 24.9 %collective-permute-start.10 = (bf16[512,1,256]{0,1,2:T(2,128)(2,1)S(1)}, bf16[512,1,256]{0,1,2:T(2,128)(2,1)S(1)}, u32[]{:S(2)}, u32[]{:S(2)}) collective-permute-start(bf16[512,1,256]{0,1,2:T(2,128)(2,1)S(1)} %slice.223), channel_id=1, source_target_pairs={{4,0},{8,4},{12,8},{5,1},{9,5},{13,9},{6,2},{10,6},{14,10},{7,3},{... | collective-permute-start | bytes 786440 | tf_op jit(solution)/shard_map/ppermute | solution.py:16
  628.2 15.1 %slice-start.5 = ((s8[16777216]{0:T(1024)(128)(4,1)}), s8[4194304]{0:T(1024)(128)(4,1)S(1)}, s32[]{:S(2)}) async-start(s8[16777216]{0:T(1024)(128)(4,1)} %bitcast.61), calls=%async_computation.6 | async-start | bytes 8388608
  628.2 15.1 %slice-start.6 = ((s8[16777216]{0:T(1024)(128)(4,1)}), s8[4194304]{0:T(1024)(128)(4,1)S(1)}, s32[]{:S(2)}) async-start(s8[16777216]{0:T(1024)(128)(4,1)} %bitcast.61), calls=%async_computation.7 | async-start | bytes 8388608
  628.2 15.1 %slice-start.7 = ((s8[16777216]{0:T(1024)(128)(4,1)}), s8[4194304]{0:T(1024)(128)(4,1)S(1)}, s32[]{:S(2)}) async-start(s8[16777216]{0:T(1024)(128)(4,1)} %bitcast.61), calls=%async_computation.8 | async-start | bytes 8388608
  628.2 23.0 %collective-permute-start.11 = (f32[512,32,1]{0,1,2:T(8,128)S(1)}, f32[512,32,1]{0,1,2:T(8,128)S(1)}, u32[]{:S(2)}, u32[]{:S(2)}) collective-permute-start(f32[512,32,1]{0,1,2:T(8,128)S(1)} %slice.190), channel_id=1, source_target_pairs={{1,0},{2,1},{3,2},{5,4},{6,5},{7,6},{9,8},{10,9},{11,10},{13,12},{... | collective-permute-start | bytes 196616 | tf_op jit(solution)/shard_map/ppermute | solution.py:16
  757.1 59.6 %collective-permute-start.12 = (bf16[512,1,256]{0,1,2:T(2,128)(2,1)S(1)}, bf16[512,1,256]{0,1,2:T(2,128)(2,1)S(1)}, u32[]{:S(2)}, u32[]{:S(2)}) collective-permute-start(bf16[512,1,256]{0,1,2:T(2,128)(2,1)S(1)} %slice.222), channel_id=1, source_target_pairs={{0,4},{4,8},{8,12},{1,5},{5,9},{9,13},{2,6},{6,10},{10,14},{3,7},{... | collective-permute-start | bytes 786440 | tf_op jit(solution)/shard_map/ppermute | solution.py:16
  762.0 55.3 %collective-permute-start.13 = (f32[512,32,1]{0,1,2:T(8,128)S(1)}, f32[512,32,1]{0,1,2:T(8,128)S(1)}, u32[]{:S(2)}, u32[]{:S(2)}) collective-permute-start(f32[512,32,1]{0,1,2:T(8,128)S(1)} %slice.195), channel_id=1, source_target_pairs={{0,1},{1,2},{2,3},{4,5},{5,6},{6,7},{8,9},{9,10},{10,11},{12,13},{... | collective-permute-start | bytes 196616 | tf_op jit(solution)/shard_map/ppermute | solution.py:16
  817.3 54.7 %copy-start.1 = (bf16[224,512]{1,0:T(8,128)(2,1)S(1)}, bf16[224,512]{1,0:T(8,128)(2,1)}, u32[]{:S(2)}) copy-start(bf16[224,512]{1,0:T(8,128)(2,1)} %param.7) | copy-start | bytes 688132
  (4 other events, 32.7 us)
Sparse Core Ops, SparseCore 0:
  41.9 177.8 all-reduce.1
where the time goes:
time: 897 us; the launch traced here: 879 us
  other arithmetic  413 us (46%)
  local copies, waits for them, and re-layouts  356 us (40%)
  starting transfers between devices  42.5 us (5%)
  waiting for transfers between devices  30.4 us (3%)
  matrix products  22.5 us (3%)
  between operations  14.9 us (2%)
    unnamed x49, local copies, waits for them, and re-layouts  164 us
    min x3, other arithmetic, on_device(): dual = jnp.clip(dual + 0.5 * jnp.stack([down, right]), -1.0, 1.0)  132 us
    sub x3, other arithmetic, inner_field(): return start - 0.25 * (current[0] - first_prev + (current[1] - second_prev))  117 us
    another operation x3, other arithmetic, on_device(): dual = jnp.clip(dual + 0.5 * jnp.stack([down, right]), -1.0, 1.0)  83.1 us
    squeeze x3, local copies, waits for them, and re-layouts, inner_field(): return start - 0.25 * (current[0] - first_prev + (current[1] - second_prev))  51.7 us
    slice x4, local copies, waits for them, and re-layouts, inner_field(): second_prev = jnp.concatenate([left, current[1][:, :, :width - 1]], axis=2)  47.6 us
    ppermute x14, starting transfers between devices, shifted(): return lax.ppermute(array, axis, pairs)  42.5 us
    max x1, other arithmetic, on_device(): abund_next = jnp.maximum(final - 0.02, 0.0)  34.5 us
  transfers between devices with their start and end apart: 15, of which 1 were waited for; matrix products, arithmetic and copies ran while one was open for 33% of the time, Pallas kernels for 0%

commit v1 on v0

v1 whole, which is shorter than its diff:
```python
import functools

import jax
import jax.numpy as jnp
from jax import lax
from jax.experimental import pallas as pl
from jax.experimental.pallas import tpu as pltpu
from jax.sharding import PartitionSpec as P

PASSES = 3
HALO = PASSES + 1
LANES = 128
BLOCK = 16


def shifted(array, axis, by):
    length = lax.axis_size(axis)
    pairs = [(i, i + by) for i in range(length) if 0 <= i + by < length]
    return lax.ppermute(array, axis, pairs)


def row_halo(array):
    height = array.shape[-2]
    below = shifted(array[..., :HALO, :], "row", -1)
    above = shifted(array[..., height - HALO :, :], "row", 1)
    return jnp.concatenate([below, above], axis=-2)


def col_halo(array, rows):
    width = array.shape[-1]

    def edge(at):
        cut = jnp.concatenate([array[..., at : at + HALO], rows[..., at : at + HALO]], axis=-2)
        return jnp.moveaxis(cut, -3, -1)

    right = shifted(edge(0), "col", -1)
    left = shifted(edge(width - HALO), "col", 1)
    gap = jnp.zeros(right.shape[:-2] + (LANES - 2 * HALO,) + right.shape[-1:], right.dtype)
    both = jnp.concatenate([right, gap, left], axis=-2)
    return jnp.moveaxis(both, -1, -3)


def step_kernel(start_ref, dual_ref, sr_ref, sc_ref, dr_ref, dc_ref, keep_ref, out_ref, dual_out_ref):
    _, height, width = start_ref.shape
    keep0 = keep_ref[0]
    keep1 = keep_ref[1]
    tall, wide = keep0.shape

    def extended(main, rows, cols):
        cols = cols.astype(jnp.float32)
        upper = jnp.concatenate([main, cols[:height]], axis=1)
        lower = jnp.concatenate([rows.astype(jnp.float32), cols[height:]], axis=1)
        return jnp.concatenate([upper, lower], axis=0)

    def one(i, carry):
        start = extended(start_ref[i], sr_ref[i], sc_ref[i])
        q0 = extended(dual_ref[0, i], dr_ref[0, i], dc_ref[0, i]) * keep0
        q1 = extended(dual_ref[1, i], dr_ref[1, i], dc_ref[1, i]) * keep1

        def field(q0, q1):
            return start - 0.25 * (q0 - pltpu.roll(q0, 1, 0) + (q1 - pltpu.roll(q1, 1, 1)))

        for _ in range(PASSES):
            z = field(q0, q1)
            half = 0.5 * z
            down = pltpu.roll(half, tall - 1, 0) - half
            right = pltpu.roll(half, wide - 1, 1) - half
            q0 = jnp.clip(q0 + down * keep0, -1.0, 1.0)
            q1 = jnp.clip(q1 + right * keep1, -1.0, 1.0)
        final = field(q0, q1)
        out_ref[i] = jnp.maximum(final[:height, :width] - 0.02, 0.0)
        dual_out_ref[0, i] = q0[:height, :width]
        dual_out_ref[1, i] = q1[:height, :width]
        return carry

    lax.fori_loop(0, start_ref.shape[0], one, 0)


def on_device(abundance, duals, reflectance, library):
    maps, height, width = abundance.shape
    total_rows = height * lax.axis_size("row")
    total_cols = width * lax.axis_size("col")
    tall, wide = height + 2 * HALO, width + LANES
    r = lax.broadcasted_iota(jnp.int32, (tall, wide), 0)
    c = lax.broadcasted_iota(jnp.int32, (tall, wide), 1)
    r = jnp.where(r >= tall - HALO, r - tall, r) + lax.axis_index("row") * height
    c = jnp.where(c >= wide - HALO, c - wide, c) + lax.axis_index("col") * width
    keep = jnp.stack([(r >= 0) & (r < total_rows - 1), (c >= 0) & (c < total_cols - 1)]).astype(jnp.float32)

    dual_rows = row_halo(duals.astype(jnp.bfloat16))
    dual_cols = col_halo(duals.astype(jnp.bfloat16), dual_rows)
    partial = jnp.einsum("bm,mhw->bhw", library, abundance.astype(jnp.bfloat16), preferred_element_type=jnp.float32)
    axis = "lib"
    count = lax.axis_size(axis)
    if count == 2:
        other = lax.ppermute(partial.astype(jnp.bfloat16), axis, [(0, 1), (1, 0)])
        total = partial + other.astype(jnp.float32)
    else:
        total = lax.psum(partial, axis)
    resid = (total - reflectance.astype(jnp.float32)).astype(jnp.bfloat16)
    descent = jnp.einsum("bm,bhw->mhw", library, resid, preferred_element_type=jnp.float32)
    start = abundance - 0.1 * descent
    narrow = start.astype(jnp.bfloat16)
    start_rows = row_halo(narrow)
    start_cols = col_halo(narrow, start_rows)

    block = BLOCK
    while maps % block:
        block //= 2
    one = lambda *dims: pl.BlockSpec((block,) + dims, lambda i: (i, 0, 0))
    two = lambda *dims: pl.BlockSpec((2, block) + dims, lambda i: (0, i, 0, 0))
    return pl.pallas_call(
        step_kernel,
        grid=(maps // block,),
        out_shape=(
            jax.ShapeDtypeStruct(abundance.shape, jnp.float32),
            jax.ShapeDtypeStruct(duals.shape, jnp.float32),
        ),
        in_specs=[
            one(height, width),
            two(height, width),
            one(2 * HALO, width),
            one(tall, LANES),
            two(2 * HALO, width),
            two(tall, LANES),
            pl.BlockSpec((2, tall, wide), lambda i: (0, 0, 0)),
        ],
        out_specs=(one(height, width), two(height, width)),
        compiler_params=pltpu.CompilerParams(
            dimension_semantics=("arbitrary",), vmem_limit_bytes=48 * 1024 * 1024
        ),
    )(start, duals, start_rows, start_cols, dual_rows, dual_cols, keep)


def solution(mesh):
    placed = (
        P("lib", "row", "col"),
        P(None, "lib", "row", "col"),
        P(None, "row", "col"),
        P(None, "lib"),
    )
    return jax.shard_map(
        on_device,
        mesh=mesh,
        in_specs=placed,
        out_specs=(P("lib", "row", "col"), P(None, "lib", "row", "col")),
        check_vma=False,
    )
```

time: 897 us -> 559 us (0.62); the launches traced: 879 us -> 553 us
  other arithmetic: 413 us -> 77.8 us
  Pallas kernels: 0 us -> 295 us
  local copies, waits for them, and re-layouts: 356 us -> 107 us
  waiting for transfers between devices: 30.4 us -> 13.9 us
  starting transfers between devices: 42.5 us -> 28.1 us
  between operations: 14.9 us -> 1.09 us
    pallas_call x0 -> x1, Pallas kernels: none -> 295 us  [on_device(): pl.pallas_call(step_kernel, grid=(maps // block,), out_shape=(jax.ShapeDt...]
    unnamed x49 -> x8, local copies, waits for them, and re-layouts: 164 us -> 7.49 us
    min x3 -> x0, other arithmetic: 132 us -> none  [on_device(): dual = jnp.clip(dual + 0.5 * jnp.stack([down, right]), -1.0, 1.0)]
    sub x3 -> x2, other arithmetic: 117 us -> 0.01 us  [the longest x1 0.01 us: on_device(): c = jnp.where(c >= wide - HALO, c - wide, c) + lax.axis_index('col') * width]
    slice x25 -> x12, local copies, waits for them, and re-layouts: 140 us -> 55.4 us  [the longest x6 45.4 us: edge(): array[..., at:at + HALO]]
    another operation x3 -> x0, other arithmetic: 83.1 us -> none  [on_device(): dual = jnp.clip(dual + 0.5 * jnp.stack([down, right]), -1.0, 1.0)]
    squeeze x3 -> x0, local copies, waits for them, and re-layouts: 51.7 us -> none  [inner_field(): return start - 0.25 * (current[0] - first_prev + (current[1] - second_prev))]
    max x1 -> x0, other arithmetic: 34.5 us -> none  [on_device(): abund_next = jnp.maximum(final - 0.02, 0.0)]
  transfers between devices with their start and end apart: 15 -> 9, of which waited for: 1 -> 3; matrix products, arithmetic and copies ran while one was open for 33% -> 20% of each run, Pallas kernels for 0% -> 0%
where the time goes in v1:
time: 559 us; the launch traced here: 553 us
  Pallas kernels  295 us (53%)
  local copies, waits for them, and re-layouts  107 us (19%)
  other arithmetic  77.8 us (14%)
  matrix products  29.7 us (5%)
  starting transfers between devices  28.1 us (5%)
  waiting for transfers between devices  13.9 us (2%)
    pallas_call x1, Pallas kernels, on_device(): pl.pallas_call(step_kernel, grid=(maps // block,), out_shape=(jax.ShapeDt...  295 us
    slice x6, local copies, waits for them, and re-layouts, edge(): array[..., at:at + HALO]  45.4 us
    ppermute x8, starting transfers between devices, shifted(): return lax.ppermute(array, axis, pairs)  26 us
    transpose x2, other arithmetic, col_halo(): return jnp.moveaxis(both, -1, -3)  24.7 us
    ppermute x4, local copies, waits for them, and re-layouts, shifted(): return lax.ppermute(array, axis, pairs)  24 us
    dot_general x1, matrix products, on_device(): jnp.einsum('bm,bhw->mhw', library, resid, preferred_element_type=jnp.floa...  19.8 us
    dot_general x1, local copies, waits for them, and re-layouts, on_device(): jnp.einsum('bm,bhw->mhw', library, resid, preferred_element_type=jnp.floa...  19.8 us
    convert_element_type x1, other arithmetic, on_device(): narrow = start.astype(jnp.bfloat16)  17.5 us
  transfers between devices with their start and end apart: 9, of which 3 were waited for; matrix products, arithmetic and copies ran while one was open for 20% of the time, Pallas kernels for 0%

profile of v1, /device:TPU:1, one launch (start us, length us, event | category | flops | bytes accessed | tf_op | source)
XLA Modules:
  0.0 552.5 jit_solution(1150980499527438538)
XLA Ops:
  0.6 6.6 %convert_element_type.25 = bf16[512,32,256]{2,1,0:T(8,128)(2,1)S(1)} convert(f32[512,32,256]{2,1,0:T(8,128)} %param.4) | non-fusion elementwise | flops 4194304 | bytes 25165824 | tf_op jit(solution)/shard_map/convert_element_type | solution.py:92
  7.3 9.9 %fusion.21 = (bf16[224,32,256]{2,0,1:T(8,128)(2,1)}, f32[224,32,256]{2,0,1:T(8,128)}) fusion(bf16[512,32,256]{2,1,0:T(8,128)(2,1)S(1)} %convert_element_type.25, bf16[224,512]{1,0:T(8,128)(2,1)S(1)} %copy-done), kind=kOutput, calls=%fused_computation.46 | convolution fusion | flops 1880883200 | bytes 19628032 | tf_op jit(solution)/shard_map/bm,mhw->bhw/dot_general | solution.py:92
  19.2 12.1 %convert_element_type.31 = bf16[2,512,32,256]{3,2,1,0:T(8,128)(2,1)S(1)} convert(f32[2,512,32,256]{3,2,1,0:T(8,128)} %dual_ref.1) | non-fusion elementwise | flops 8388608 | bytes 50331648 | tf_op jit(solution)/shard_map/convert_element_type | solution.py:90
  31.4 6.2 %copy-done.2 = bf16[2,512,32,256]{3,2,1,0:T(8,128)(2,1)} copy-done((bf16[2,512,32,256]{3,2,1,0:T(8,128)(2,1)}, bf16[2,512,32,256]{3,2,1,0:T(8,128)(2,1)S(1)}, u32[]{:S(2)}) %copy-start.2) | copy-done | bytes 16777240
  37.5 3.5 fusion.18
  42.3 5.6 %collective-permute-start.6 = (bf16[2,512,4,256]{3,2,1,0:T(4,128)(2,1)}, bf16[2,512,4,256]{3,2,1,0:T(4,128)(2,1)}, u32[]{:S(2)}, u32[]{:S(2)}) collective-permute-start(bf16[2,512,4,256]{3,2,1,0:T(4,128)(2,1)} %get-tuple-element.7), channel_id=1, source_target_pairs={{0,4},{4,8},{8,12},{1,5},{5,9},{9,13},{2,6},{6,10},{10,14},{3,7},{... | collective-permute-start | bytes 6291464 | tf_op jit(solution)/shard_map/ppermute | solution.py:19
  47.9 12.7 %fusion.17 = (bf16[2,512,32,4]{3,2,1,0:T(8,128)(2,1)}, bf16[2,512,32,4]{3,2,1,0:T(8,128)(2,1)}) fusion(bf16[2,512,32,256]{3,2,1,0:T(8,128)(2,1)} %copy-done.2), kind=kLoop, calls=%fused_computation.42 | loop fusion | bytes 1048576 | tf_op jit(solution)/shard_map/slice | solution.py:33
  60.6 9.0 %copy.18 = bf16[2,512,32,4]{1,2,3,0:T(8,128)(2,1)S(1)} copy(bf16[2,512,32,4]{3,2,1,0:T(8,128)(2,1)} %get-tuple-element.4) | data formatting | bytes 524288 | tf_op jit(solution)/shard_map/slice | solution.py:33
  69.6 9.0 %copy.20 = bf16[2,512,32,4]{1,2,3,0:T(8,128)(2,1)S(1)} copy(bf16[2,512,32,4]{3,2,1,0:T(8,128)(2,1)} %get-tuple-element.5) | data formatting | bytes 524288 | tf_op jit(solution)/shard_map/slice | solution.py:33
  78.8 10.6 %collective-permute-done.5 = bf16[2,512,4,256]{3,2,1,0:T(4,128)(2,1)S(1)} collective-permute-done((bf16[2,512,4,256]{3,2,1,0:T(4,128)(2,1)}, bf16[2,512,4,256]{3,2,1,0:T(4,128)(2,1)S(1)}, u32[]{:S(2)}, u32[]{:S(2)}) %collective-permute-start.5) | collective-permute-done | bytes 2097184 | tf_op jit(solution)/shard_map/ppermute | solution.py:19
  90.7 5.3 fusion.4
  96.1 2.8 copy.19
  100.4 4.7 collective-permute-start.8
  105.1 2.4 collective-permute-start.7
  107.6 4.9 pad_maximum_fusion.dr_ref
  113.5 7.4 %copy.22 = bf16[2,40,4,512]{2,1,3,0:T(8,128)(2,1)} copy(bf16[2,40,4,512]{3,1,2,0:T(8,128)(2,1)S(1)} %collective-permute-done.7) | data formatting | bytes 655360 | tf_op jit(solution)/shard_map/ppermute | solution.py:19
  120.9 7.5 %copy.23 = bf16[2,40,4,512]{2,1,3,0:T(8,128)(2,1)} copy(bf16[2,40,4,512]{3,1,2,0:T(8,128)(2,1)S(1)} %collective-permute-done.8) | data formatting | bytes 655360 | tf_op jit(solution)/shard_map/ppermute | solution.py:19
  128.4 19.8 %fusion.2 = f32[32,256,512]{2,1,0:T(8,128)} fusion(f32[224,32,256]{2,0,1:T(8,128)} %get-tuple-element.17, bf16[224,32,256]{2,0,1:T(8,128)(2,1)} %collective-permute-done, bf16[224,32,256]{2,1,0:T(8,128)(2,1)} %param.6, bf16[224,512]{1,0:T(8,128)(2,1)S(1)} %copy-done), kind=kOutput, calls=%fused_computation.11 | convolution fusion | flops 1888223232 | bytes 31686656 | tf_op jit(solution)/shard_map/bm,bhw->mhw/dot_general | solution.py:101
  148.3 19.8 %copy.11 = f32[32,256,512]{1,0,2:T(8,128)} copy(f32[32,256,512]{2,1,0:T(8,128)} %fusion.2) | data formatting | bytes 33554432 | tf_op jit(solution)/shard_map/bm,bhw->mhw/dot_general | solution.py:101
  168.1 17.5 %fusion.16 = (bf16[512,32,256]{2,1,0:T(8,128)(2,1)S(1)}, f32[512,32,256]{2,1,0:T(8,128)}) fusion(f32[512,32,256]{2,1,0:T(8,128)} %param.4, f32[32,256,512]{1,0,2:T(8,128)} %copy.11), kind=kLoop, calls=%fused_computation.41 | loop fusion | flops 12582912 | bytes 58720256 | tf_op jit(solution)/shard_map/convert_element_type | solution.py:103
  187.7 5.7 %collective-permute-start.2 = (bf16[512,4,256]{2,1,0:T(4,128)(2,1)S(1)}, bf16[512,4,256]{2,1,0:T(4,128)(2,1)}, u32[]{:S(2)}, u32[]{:S(2)}) collective-permute-start(bf16[512,4,256]{2,1,0:T(4,128)(2,1)S(1)} %get-tuple-element.11), channel_id=1, source_target_pairs={{0,4},{4,8},{8,12},{1,5},{5,9},{9,13},{2,6},{6,10},{10,14},{3,7},{... | collective-permute-start | bytes 3145736 | tf_op jit(solution)/shard_map/ppermute | solution.py:19
  193.4 15.1 %maximum_bitcast_fusion.dc_ref = bf16[2,512,40,128]{3,2,1,0:T(8,128)(2,1)} fusion(bf16[2,40,4,512]{2,1,3,0:T(8,128)(2,1)} %copy.23, bf16[2,40,4,512]{2,1,3,0:T(8,128)(2,1)} %copy.22, bf16[128]{0:T(256)(128)(2,1)S(1)} %pad.12.clone), kind=kLoop, calls=%fused_computation.1 | loop fusion | flops 31457280 | bytes 11141376 | tf_op jit(solution)/shard_map/transpose | solution.py:40
  208.4 4.4 fusion.19
  212.9 4.8 copy.12
  217.7 5.5 copy.14
  223.2 2.6 fusion.6
  228.9 2.9 collective-permute-start.4
  236.2 2.3 collective-permute-done.3
  238.4 4.2 copy.16
  242.6 4.9 copy.17
  247.5 9.6 %maximum_bitcast_fusion.1.sc_ref = bf16[512,40,128]{2,1,0:T(8,128)(2,1)} fusion(bf16[40,4,512]{1,0,2:T(8,128)(2,1)} %copy.17, bf16[40,4,512]{1,0,2:T(8,128)(2,1)} %copy.16, bf16[128]{0:T(256)(128)(2,1)S(1)} %pad.12.clone), kind=kLoop, calls=%fused_computation.10 | loop fusion | flops 15728640 | bytes 5570816 | tf_op jit(solution)/shard_map/transpose | solution.py:40
  257.2 295.1 %shard_map.59 = (f32[512,32,256]{2,1,0:T(8,128)}, f32[2,512,32,256]{3,2,1,0:T(8,128)}) custom-call(f32[512,32,256]{2,1,0:T(8,128)} %get-tuple-element.3.start_ref, f32[2,512,32,256]{3,2,1,0:T(8,128)} %dual_ref.1, bf16[512,8,256]{2,1,0:T(8,128)(2,1)S(1)} %pad_maximum_fusion.1.sr_ref, bf16[512,40,128]{2,1,0:T(8,128)(2,1)} %maximum_bitcast_fusion.1.sc_ref, ...), custom_call_target="tpu_custom_call" | custom-call | tf_op jit(solution)/shard_map/pallas_call | solution.py:112
  (35 shorter events, 17.0 us)
Async XLA Ops:
  0.6 6.6 %copy-start = (bf16[224,512]{1,0:T(8,128)(2,1)S(1)}, bf16[224,512]{1,0:T(8,128)(2,1)}, u32[]{:S(2)}) copy-start(bf16[224,512]{1,0:T(8,128)(2,1)} %param.7) | copy-start | bytes 688132
  17.2 111.3 %collective-permute-start = (bf16[224,32,256]{2,0,1:T(8,128)(2,1)}, bf16[224,32,256]{2,0,1:T(8,128)(2,1)}, u32[]{:S(2)}, u32[]{:S(2)}) collective-permute-start(bf16[224,32,256]{2,0,1:T(8,128)(2,1)} %get-tuple-element.16), channel_id=1, source_target_pairs={{0,16},{16,0},{1,17},{17,1},{2,18},{18,2},{3,19},{19,3},{4,20},{20... | collective-permute-start | bytes 11010056 | tf_op jit(solution)/shard_map/ppermute | solution.py:96
  31.4 6.2 %copy-start.2 = (bf16[2,512,32,256]{3,2,1,0:T(8,128)(2,1)}, bf16[2,512,32,256]{3,2,1,0:T(8,128)(2,1)S(1)}, u32[]{:S(2)}) copy-start(bf16[2,512,32,256]{3,2,1,0:T(8,128)(2,1)S(1)} %convert_element_type.31) | copy-start | bytes 50331652
  41.0 48.4 %collective-permute-start.5 = (bf16[2,512,4,256]{3,2,1,0:T(4,128)(2,1)}, bf16[2,512,4,256]{3,2,1,0:T(4,128)(2,1)S(1)}, u32[]{:S(2)}, u32[]{:S(2)}) collective-permute-start(bf16[2,512,4,256]{3,2,1,0:T(4,128)(2,1)} %get-tuple-element.6), channel_id=1, source_target_pairs={{4,0},{8,4},{12,8},{5,1},{9,5},{13,9},{6,2},{10,6},{14,10},{7,3},{... | collective-permute-start | bytes 6291464 | tf_op jit(solution)/shard_map/ppermute | solution.py:19
  42.3 48.5 %collective-permute-start.6 = (bf16[2,512,4,256]{3,2,1,0:T(4,128)(2,1)}, bf16[2,512,4,256]{3,2,1,0:T(4,128)(2,1)}, u32[]{:S(2)}, u32[]{:S(2)}) collective-permute-start(bf16[2,512,4,256]{3,2,1,0:T(4,128)(2,1)} %get-tuple-element.7), channel_id=1, source_target_pairs={{0,4},{4,8},{8,12},{1,5},{5,9},{9,13},{2,6},{6,10},{10,14},{3,7},{... | collective-permute-start | bytes 6291464 | tf_op jit(solution)/shard_map/ppermute | solution.py:19
  89.4 1.3 copy-start.3
  100.4 20.6 %collective-permute-start.8 = (bf16[2,40,4,512]{3,1,2,0:T(8,128)(2,1)S(1)}, bf16[2,40,4,512]{3,1,2,0:T(8,128)(2,1)S(1)}, u32[]{:S(2)}, u32[]{:S(2)}) collective-permute-start(bf16[2,40,4,512]{3,1,2,0:T(8,128)(2,1)S(1)} %maximum_bitcast_fusion.3), channel_id=1, source_target_pairs={{0,1},{1,2},{2,3},{4,5},{5,6},{6,7},{8,9},{9,10},{10,11},{12,13},{... | collective-permute-start | bytes 983048 | tf_op jit(solution)/shard_map/ppermute | solution.py:19
  105.1 8.4 %collective-permute-start.7 = (bf16[2,40,4,512]{3,1,2,0:T(8,128)(2,1)S(1)}, bf16[2,40,4,512]{3,1,2,0:T(8,128)(2,1)S(1)}, u32[]{:S(2)}, u32[]{:S(2)}) collective-permute-start(bf16[2,40,4,512]{3,1,2,0:T(8,128)(2,1)S(1)} %maximum_bitcast_fusion.2), channel_id=1, source_target_pairs={{1,0},{2,1},{3,2},{5,4},{6,5},{7,6},{9,8},{10,9},{11,10},{13,12},{... | collective-permute-start | bytes 983048 | tf_op jit(solution)/shard_map/ppermute | solution.py:19
  186.4 36.8 %collective-permute-start.1 = (bf16[512,4,256]{2,1,0:T(4,128)(2,1)S(1)}, bf16[512,4,256]{2,1,0:T(4,128)(2,1)S(1)}, u32[]{:S(2)}, u32[]{:S(2)}) collective-permute-start(bf16[512,4,256]{2,1,0:T(4,128)(2,1)S(1)} %get-tuple-element.10), channel_id=1, source_target_pairs={{4,0},{8,4},{12,8},{5,1},{9,5},{13,9},{6,2},{10,6},{14,10},{7,3},{... | collective-permute-start | bytes 3145736 | tf_op jit(solution)/shard_map/ppermute | solution.py:19
  187.7 35.5 %collective-permute-start.2 = (bf16[512,4,256]{2,1,0:T(4,128)(2,1)S(1)}, bf16[512,4,256]{2,1,0:T(4,128)(2,1)}, u32[]{:S(2)}, u32[]{:S(2)}) collective-permute-start(bf16[512,4,256]{2,1,0:T(4,128)(2,1)S(1)} %get-tuple-element.11), channel_id=1, source_target_pairs={{0,4},{4,8},{8,12},{1,5},{5,9},{9,13},{2,6},{6,10},{10,14},{3,7},{... | collective-permute-start | bytes 3145736 | tf_op jit(solution)/shard_map/ppermute | solution.py:19
  228.9 13.8 %collective-permute-start.4 = (bf16[40,4,512]{2,0,1:T(8,128)(2,1)}, bf16[40,4,512]{2,0,1:T(8,128)(2,1)}, u32[]{:S(2)}, u32[]{:S(2)}) collective-permute-start(bf16[40,4,512]{2,0,1:T(8,128)(2,1)} %maximum_bitcast_fusion.5), channel_id=1, source_target_pairs={{0,1},{1,2},{2,3},{4,5},{5,6},{6,7},{8,9},{9,10},{10,11},{12,13},{... | collective-permute-start | bytes 491528 | tf_op jit(solution)/shard_map/ppermute | solution.py:19
  231.8 6.6 %collective-permute-start.3 = (bf16[40,4,512]{2,0,1:T(8,128)(2,1)S(1)}, bf16[40,4,512]{2,0,1:T(8,128)(2,1)S(1)}, u32[]{:S(2)}, u32[]{:S(2)}) collective-permute-start(bf16[40,4,512]{2,0,1:T(8,128)(2,1)S(1)} %maximum_bitcast_fusion.4), channel_id=1, source_target_pairs={{1,0},{2,1},{3,2},{5,4},{6,5},{7,6},{9,8},{10,9},{11,10},{13,12},{... | collective-permute-start | bytes 491528 | tf_op jit(solution)/shard_map/ppermute | solution.py:19
  257.1 295.1 %copy-start.1 = (bf16[224,512]{1,0:T(8,128)(2,1)S(1)}, bf16[224,512]{1,0:T(8,128)(2,1)}, u32[]{:S(2)}) copy-start(bf16[224,512]{1,0:T(8,128)(2,1)} %param.7) | copy-start | bytes 688132
